TPU v7x, 32 devices: a whole 2x2x4 slice. The times are simulated.
32 devices in a mesh: trial: 2 (over core), bank: 4 (over y, x), zero: 4 (over z).
Axes of the slice: x: 2, y: 2, z: 4, core: 2. Of those that a mesh axis runs over, the one named last changes fastest.
Arguments:
- w_gate: float32 [128, 2048, 1024], P(('trial', 'bank'), 'zero'), parts along dimension 0, may hold values from -0.1875 to 0.1875
- w_up: float32 [128, 2048, 1024], P(('trial', 'bank'), 'zero'), parts along dimension 0, may hold values from -0.1875 to 0.1875
- router_weight: float32 [4096, 64], P(('trial', 'zero'), 'bank'), parts along dimension 0, may hold values from -0.125 to 0.125
- router_gain: float32 [4096], P(('trial', 'zero')), parts along dimension 0, may hold values from 0.25 to 1.75
Outputs:
- serve_gate: bfloat16 [128, 2048, 1024], P(('trial', 'bank'), None, 'zero'), parts along dimension 0
- serve_up: bfloat16 [128, 2048, 1024], P(('trial', 'bank'), None, 'zero'), parts along dimension 0
- scale_gate: float32 [128, 1024], P(('trial', 'bank'), 'zero'), parts along dimension 0
- scale_up: float32 [128, 1024], P(('trial', 'bank'), 'zero'), parts along dimension 0
- serve_router: bfloat16 [4096, 64], P('trial'), parts along dimension 0
There are 2 independent parts, one for each index of `trial`. A program takes and returns all parts, laid end to end along the dimension named above; each array names one. Nothing has to cross between parts.
All inputs are finite; a program needn't handle non-finite values. Where the computation divides by a largest or mean magnitude, that divisor is 1e-20 or more.
Results may differ from a plain program's by a relative error of at most 0.001.
Values may be sent and summed in bfloat16 or wider, within the bound.
A program may use at most 192 MiB of HBM per device.

v0:
```python
import jax
import jax.numpy as jnp
from jax import lax
from jax.sharding import PartitionSpec as P

D_MODEL = 2048


def local(w_gate, w_up, router_weight, router_gain):
    total_gate, total_up = lax.psum(
        (jnp.sum(jnp.abs(w_gate), axis=1), jnp.sum(jnp.abs(w_up), axis=1)), "zero"
    )
    scale_gate = total_gate / D_MODEL
    scale_up = total_up / D_MODEL
    narrow_gate, narrow_up = (
        (w_gate / jnp.expand_dims(scale_gate, 1)).astype(jnp.bfloat16),
        (w_up / jnp.expand_dims(scale_up, 1)).astype(jnp.bfloat16),
    )
    serve_gate, serve_up = (
        lax.all_to_all(narrow_gate, "zero", split_axis=2, concat_axis=1, tiled=True),
        lax.all_to_all(narrow_up, "zero", split_axis=2, concat_axis=1, tiled=True),
    )
    scale_gate = lax.dynamic_slice_in_dim(
        scale_gate, lax.axis_index("zero") * serve_gate.shape[2], serve_gate.shape[2], axis=1
    )
    scale_up = lax.dynamic_slice_in_dim(
        scale_up, lax.axis_index("zero") * serve_up.shape[2], serve_up.shape[2], axis=1
    )
    part_router = (router_weight * router_gain[:, None]).astype(jnp.bfloat16)
    row_router = lax.all_gather(part_router, "zero", axis=0, tiled=True)
    serve_router = lax.all_gather(row_router, "bank", axis=1, tiled=True)
    return (serve_gate, serve_up, scale_gate, scale_up, serve_router)


def solution(mesh):
    placed = (
        P(("trial", "bank"), "zero", None),
        P(("trial", "bank"), "zero", None),
        P(("trial", "zero"), "bank"),
        P(("trial", "zero")),
    )
    return jax.shard_map(
        local,
        mesh=mesh,
        in_specs=placed,
        out_specs=(
            P(("trial", "bank"), None, "zero"),
            P(("trial", "bank"), None, "zero"),
            P(("trial", "bank"), "zero"),
            P(("trial", "bank"), "zero"),
            P("trial", None),
        ),
        check_vma=False,
    )
```

profile of v0, /device:TPU:0, one launch (start us, length us, event | category | flops | bytes accessed | tf_op | source)
XLA Modules:
  0.0 899.1 jit_solution(11479732921372934390)
XLA Ops:
  7.2 0.0 all-reduce.3.cloned.1.call-start
  7.2 22.1 %abs_reduce_fusion = (f32[16,1024]{1,0:T(8,128)}, f32[16,1024]{1,0:T(8,128)}) fusion(f32[16,512,1024]{2,1,0:T(8,128)} %param.5, f32[16,512,1024]{2,1,0:T(8,128)} %param.4), kind=kLoop, calls=%fused_computation.1 | loop fusion | flops 33521664 | bytes 67239936 | tf_op jit(solution)/shard_map/reduce_sum | solution.py:11
  29.3 0.0 all-reduce.3.cloned.1.call-update
  29.3 34.3 %copy.15 = f32[16,512,1024]{1,0,2:T(8,128)} copy(f32[16,512,1024]{2,1,0:T(8,128)} %param.5) | data formatting | bytes 67108864 | tf_op args[1]
  63.6 3.3 all-reduce.3.cloned.1.call-done
  66.9 0.8 broadcast_multiply_fusion
  67.8 0.2 copy.14
  68.0 17.7 %divide_convert_fusion = bf16[16,512,1024]{1,0,2:T(8,128)(2,1)} fusion(f32[16,512,1024]{1,0,2:T(8,128)} %copy.15, f32[16,1024]{0,1:T(8,128)S(1)} %copy.14), kind=kLoop, calls=%fused_computation | loop fusion | flops 16777216 | bytes 50397184 | tf_op jit(solution)/shard_map/convert_element_type | solution.py:17
  85.6 7.1 all-to-all-start.1
  92.7 34.2 %copy.12 = f32[16,512,1024]{1,0,2:T(8,128)} copy(f32[16,512,1024]{2,1,0:T(8,128)} %param.4) | data formatting | bytes 67108864 | tf_op args[0]
  126.9 0.2 copy.11
  127.1 0.0 copy-start.1
  127.1 0.0 copy-start.2
  127.1 17.7 %divide_convert_fusion.1 = bf16[16,512,1024]{1,0,2:T(8,128)(2,1)} fusion(f32[16,512,1024]{1,0,2:T(8,128)} %copy.12, f32[16,1024]{0,1:T(8,128)S(1)} %copy.11), kind=kLoop, calls=%fused_computation.2 | loop fusion | flops 16777216 | bytes 50397184 | tf_op jit(solution)/shard_map/convert_element_type | solution.py:16
  144.8 308.9 %all-to-all-done.1 = bf16[16,512,1024]{1,0,2:T(8,128)(2,1)} async-done(((bf16[16,512,1024]{1,0,2:T(8,128)(2,1)}), bf16[16,512,1024]{1,0,2:T(8,128)(2,1)}, u32[]{:S(2)}, u32[]{:S(2)}) %all-to-all-start.1) | async-done | bytes 16777248 | tf_op jit(solution)/shard_map/all_to_all | solution.py:21
  453.7 7.0 all-to-all-start
  460.8 367.8 %all_gather.6 = bf16[2048,16]{0,1:T(8,128)(2,1)S(1)} all-gather(bf16[512,16]{0,1:T(8,128)(2,1)S(1)} %multiply_convert_fusion), channel_id=1, replica_groups=mesh['trial'=2,'bank'=4,'zero'=4] {'zero'}, dimensions={0}, use_global_device_ids=true | all-gather | bytes 81920 | tf_op jit(solution)/shard_map/all_gather | solution.py:30
  828.5 9.5 %all_gather.7 = bf16[2048,64]{0,1:T(8,128)(2,1)S(1)} all-gather(bf16[2048,16]{0,1:T(8,128)(2,1)S(1)} %all_gather.6), channel_id=1, replica_groups=mesh['trial'=2,'bank'=4,'zero'=4] {'bank'}, dimensions={1}, use_global_device_ids=true | all-gather | bytes 327680 | tf_op jit(solution)/shard_map/all_gather | solution.py:31
  838.0 0.6 constant_dynamic-slice_fusion
  838.6 0.6 constant_dynamic-slice_fusion.1
  839.2 26.2 %copy.16 = bf16[16,4,512,256]{3,2,1,0:T(8,128)(2,1)} copy(bf16[16,4,512,256]{2,0,3,1:T(8,128)(2,1)} %bitcast.4) | data formatting | bytes 33554432 | tf_op jit(solution)/shard_map/all_to_all | solution.py:21
  865.4 0.0 all-to-all-done
  865.4 26.2 %copy.13 = bf16[16,4,512,256]{3,2,1,0:T(8,128)(2,1)} copy(bf16[16,4,512,256]{2,0,3,1:T(8,128)(2,1)} %bitcast.1) | data formatting | bytes 33554432 | tf_op jit(solution)/shard_map/all_to_all | solution.py:20
  891.6 0.7 copy.20
  (6 shorter events, 0.0 us)
Async XLA Ops:
  7.2 59.7 %all-reduce.3.cloned.1.call-start = ((), (), s32[]{:S(2)}) async-start(), calls=%async_computation.2 | async-start | bytes 262144 | tf_op jit(solution)/shard_map/psum | solution.py:10
  85.6 368.1 %all-to-all-start.1 = ((bf16[16,512,1024]{1,0,2:T(8,128)(2,1)}), bf16[16,512,1024]{1,0,2:T(8,128)(2,1)}, u32[]{:S(2)}, u32[]{:S(2)}) async-start(bf16[16,512,1024]{1,0,2:T(8,128)(2,1)} %divide_convert_fusion), calls=%async_computation.1 | async-start | bytes 33554432 | tf_op jit(solution)/shard_map/all_to_all | solution.py:21
  92.7 34.2 %copy-start = (f32[16,1024]{1,0:T(8,128)S(1)}, f32[16,1024]{1,0:T(8,128)}, u32[]{:S(2)}) copy-start(f32[16,1024]{1,0:T(8,128)} %get-tuple-element.5) | copy-start | bytes 196612
  127.1 333.6 %copy-start.1 = (f32[512,16]{0,1:T(8,128)S(1)}, f32[512,16]{0,1:T(8,128)}, u32[]{:S(2)}) copy-start(f32[512,16]{0,1:T(8,128)} %param.6) | copy-start | bytes 98308
  127.1 333.6 %copy-start.2 = (f32[512]{0:T(512)S(1)}, f32[512]{0:T(512)}, u32[]{:S(2)}) copy-start(f32[512]{0:T(512)} %param.7) | copy-start | bytes 6148
  453.7 411.7 %all-to-all-start = ((bf16[16,512,1024]{1,0,2:T(8,128)(2,1)}), bf16[16,512,1024]{1,0,2:T(8,128)(2,1)}, u32[]{:S(2)}, u32[]{:S(2)}) async-start(bf16[16,512,1024]{1,0,2:T(8,128)(2,1)} %divide_convert_fusion.1), calls=%async_computation | async-start | bytes 33554432 | tf_op jit(solution)/shard_map/all_to_all | solution.py:20
Sparse Core Ops, SparseCore 0:
  29.4 37.4 all-reduce.2
where the time goes:
time: 902 us; the launch traced here: 899 us
  blocking collectives  377 us (42%)
  waiting for transfers between devices  312 us (35%)
  local copies, waits for them, and re-layouts  123 us (14%)
  other arithmetic  58.3 us (6%)
  starting transfers between devices  14.1 us (2%)
  between operations  14.1 us (2%)
    all_gather x1, blocking collectives, local(): row_router = lax.all_gather(part_router, 'zero', axis=0, tiled=True)  368 us
    all_to_all x1, waiting for transfers between devices, local(): lax.all_to_all(narrow_up, 'zero', split_axis=2, concat_axis=1, tiled=True)  309 us
    unnamed x9, local copies, waits for them, and re-layouts  69.1 us
    all_to_all x1, local copies, waits for them, and re-layouts, local(): lax.all_to_all(narrow_gate, 'zero', split_axis=2, concat_axis=1, tiled=True)  26.2 us
    all_to_all x1, local copies, waits for them, and re-layouts, local(): lax.all_to_all(narrow_up, 'zero', split_axis=2, concat_axis=1, tiled=True)  26.2 us
    reduce_sum x1, other arithmetic, local(): jnp.sum(jnp.abs(w_up), axis=1)  22.1 us
  transfers between devices with their start and end apart: 3, of which 2 were waited for; matrix products, arithmetic and copies ran while one was open for 13% of the time, Pallas kernels for 0%

commit v1 on v0

v1 whole, which is shorter than its diff:
```python
import functools

import jax
import jax.numpy as jnp
from jax import lax
from jax.experimental import pallas as pl
from jax.experimental.pallas import tpu as pltpu
from jax.sharding import PartitionSpec as P

MESH = pl.DeviceIdType.MESH
SLOTS = 3
STEP = 16


def plain(n, w_gate, w_up, router_weight, router_gain):
    d_model = w_gate.shape[1] * n

    def rescaled(w):
        scale = lax.psum(jnp.sum(jnp.abs(w), axis=1), "zero") / d_model
        narrow = (w / jnp.expand_dims(scale, 1)).astype(jnp.bfloat16)
        serve = lax.all_to_all(narrow, "zero", split_axis=2, concat_axis=1, tiled=True)
        width = serve.shape[2]
        return serve, lax.dynamic_slice_in_dim(scale, lax.axis_index("zero") * width, width, axis=1)

    serve_gate, scale_gate = rescaled(w_gate)
    serve_up, scale_up = rescaled(w_up)
    part = (router_weight * router_gain[:, None]).astype(jnp.bfloat16)
    row = lax.all_gather(part, "zero", axis=0, tiled=True)
    router = lax.all_gather(row, "bank", axis=1, tiled=True)
    return serve_gate, serve_up, scale_gate, scale_up, router


def kernel(
    n, banks, wg_ref, wu_ref, rw_ref, rg_ref,
    og_ref, ou_ref, sg_ref, su_ref, rt_ref,
    stage, first, sendbuf, parts, scales,
    in_sem, first_sem, own_sem, send_sem, recv_sem, x_send, x_recv, rz_send, rz_recv, rb_send, rb_recv,
):
    me = lax.axis_index("zero")
    bank = lax.axis_index("bank")
    w, o, so = (wg_ref, wu_ref), (og_ref, ou_ref), (sg_ref, su_ref)
    experts, rows, cols = wg_ref.shape
    width = cols // n
    d_model = rows * n

    for m in range(2):
        pltpu.make_async_copy(w[m].at[0], first.at[m], first_sem.at[m]).start()

    def load(m, e, slot):
        return pltpu.make_async_copy(w[m].at[e], stage.at[m, slot], in_sem.at[m, slot])

    for e in range(1, min(1 + SLOTS, experts)):
        for m in range(2):
            load(m, e, e % SLOTS).start()

    def others(axis, here, count, act):
        for p in range(count):
            @pl.when(here != p)
            def _():
                act(p)

    barrier = pltpu.get_barrier_semaphore()

    def greet(axis):
        return lambda p: pl.semaphore_signal(barrier, inc=1, device_id={axis: p}, device_id_type=MESH)

    others("zero", me, n, greet("zero"))
    others("bank", bank, banks, greet("bank"))

    def stats(src, m, e):
        def body(r, acc):
            return acc + jnp.abs(src[pl.ds(pl.multiple_of(r * 8, 8), 8), :])

        acc = lax.fori_loop(0, rows // 8, body, jnp.zeros((8, cols), jnp.float32), unroll=8)
        parts[me, e, m] = jnp.sum(acc, axis=0, keepdims=True)

    def chunk(ref, s, g):
        if g < 2:
            return ref.at[s, 0, g]
        return ref.at[s, pl.ds(1, experts - 1)]

    def swap(g, p):
        return pltpu.make_async_remote_copy(
            src_ref=chunk(parts, me, g), dst_ref=chunk(parts, me, g),
            send_sem=x_send.at[g, p], recv_sem=x_recv.at[g, me],
            device_id={"zero": p}, device_id_type=MESH,
        )

    def swapped(g, p):
        return pltpu.make_async_remote_copy(
            src_ref=chunk(parts, p, g), dst_ref=chunk(parts, p, g),
            send_sem=x_send.at[g, p], recv_sem=x_recv.at[g, p],
            device_id={"zero": p}, device_id_type=MESH,
        )

    def narrow(src, m, e):
        total = parts[0, e, m]
        for s in range(1, n):
            total = total + parts[s, e, m]
        scale = total / d_model
        scales[...] = scale
        so[m][pl.ds(e, 1), :] = scales[:, pl.ds(pl.multiple_of(me * width, width), width)]

        def body(r, carry):
            at = pl.ds(pl.multiple_of(r * STEP, STEP), STEP)
            for c in range(n):
                lanes = slice(c * width, (c + 1) * width)
                sendbuf[m, e, c, at, :] = (src[at, lanes] / scale[:, lanes]).astype(jnp.bfloat16)
            return carry

        lax.fori_loop(0, rows // STEP, body, 0, unroll=2)

    def place(ref, e, s):
        return ref.at[e, pl.ds(pl.multiple_of(s * rows, rows), rows), :]

    def keep(m, e):
        pltpu.make_async_copy(sendbuf.at[m, e, me], place(o[m], e, me), own_sem.at[m]).start()

    def send(m, e, p):
        pltpu.make_async_remote_copy(
            src_ref=sendbuf.at[m, e, p], dst_ref=place(o[m], e, me),
            send_sem=send_sem.at[m, p], recv_sem=recv_sem.at[m, me],
            device_id={"zero": p}, device_id_type=MESH,
        ).start()

    def send_at(m, e, t):
        @pl.when(me + t < n)
        def _():
            send(m, e, me + t)

        @pl.when(me - t >= 0)
        def _():
            send(m, e, me - t)

    for m in range(2):
        pltpu.make_async_copy(w[m].at[0], first.at[m], first_sem.at[m]).wait()
        stats(first.at[m], m, 0)
        if m == 0:
            pl.semaphore_wait(barrier, n - 1 + banks - 1)
        others("zero", me, n, lambda p: swap(m, p).start())

    def arrived(g):
        others("zero", me, n, lambda p: swapped(g, p).wait_recv())

    arrived(0)
    narrow(first.at[0], 0, 0)
    for t in range(1, n):
        send_at(0, 0, t)
    keep(0, 0)

    depth = rw_ref.shape[1]
    mine = pl.ds(pl.multiple_of(me * depth, depth), depth)
    rt_ref[bank, :, mine] = (rw_ref[...] * rg_ref[...]).astype(jnp.bfloat16)

    def row_copy(s, p):
        at = pl.ds(pl.multiple_of(s * depth, depth), depth)
        return pltpu.make_async_remote_copy(
            src_ref=rt_ref.at[bank, :, at], dst_ref=rt_ref.at[bank, :, at],
            send_sem=rz_send.at[p], recv_sem=rz_recv.at[s],
            device_id={"zero": p}, device_id_type=MESH,
        )

    def sizes(e, carry):
        slot = e % SLOTS
        for m in range(2):
            load(m, e, slot).wait()
            stats(stage.at[m, slot], m, e)

            @pl.when(e + SLOTS < experts)
            def _():
                load(m, e + SLOTS, slot).start()
        return carry

    lax.fori_loop(1, experts, sizes, 0)
    others("zero", me, n, lambda p: swap(2, p).start())
    for e in range(1, min(1 + SLOTS, experts)):
        for m in range(2):
            load(m, e, e % SLOTS).start()

    arrived(1)
    narrow(first.at[1], 1, 0)
    for t in range(1, n):
        send_at(1, 0, t)
    keep(1, 0)
    others("zero", me, n, lambda p: row_copy(me, p).start())

    arrived(2)

    def narrowed(e, carry):
        slot = e % SLOTS
        for m in range(2):
            load(m, e, slot).wait()
            narrow(stage.at[m, slot], m, e)

            @pl.when(e + SLOTS < experts)
            def _():
                load(m, e + SLOTS, slot).start()

            send_at(m, e, 1)
            keep(m, e)
        return carry

    lax.fori_loop(1, experts, narrowed, 0)

    def far(e, carry):
        for m in range(2):
            for t in range(2, n):
                send_at(m, e, t)
        return carry

    lax.fori_loop(1, experts, far, 0)

    others("zero", me, n, lambda p: row_copy(p, p).wait_recv())

    def column_copy(s, p):
        return pltpu.make_async_remote_copy(
            src_ref=rt_ref.at[s], dst_ref=rt_ref.at[s],
            send_sem=rb_send.at[p], recv_sem=rb_recv.at[s],
            device_id={"bank": p}, device_id_type=MESH,
        )

    others("bank", bank, banks, lambda p: column_copy(bank, p).start())
    others("bank", bank, banks, lambda p: column_copy(p, p).wait_recv())
    others("bank", bank, banks, lambda p: column_copy(bank, p).wait_send())
    others("zero", me, n, lambda p: row_copy(me, p).wait_send())
    for g in range(3):
        others("zero", me, n, lambda p: swap(g, p).wait_send())

    for m in range(2):
        def whole(s, p):
            return pltpu.make_async_remote_copy(
                src_ref=sendbuf.at[m, :, p],
                dst_ref=o[m].at[:, pl.ds(pl.multiple_of(s * rows, rows), rows), :],
                send_sem=send_sem.at[m, p], recv_sem=recv_sem.at[m, s],
                device_id={"zero": p}, device_id_type=MESH,
            )

        pltpu.make_async_copy(
            sendbuf.at[m, :, me], o[m].at[:, pl.ds(pl.multiple_of(me * rows, rows), rows), :], own_sem.at[m]
        ).wait()
        others("zero", me, n, lambda p: whole(me, p).wait_send())
        others("zero", me, n, lambda p: whole(p, p).wait_recv())


def local(n, banks, w_gate, w_up, router_weight, router_gain):
    experts, rows, cols = w_gate.shape
    width = cols // n
    depth, heads = router_weight.shape
    fits = width % 128 == 0 and rows % 16 == 0 and depth % 128 == 0 and heads % 16 == 0 and experts > 1
    if not fits:
        return plain(n, w_gate, w_up, router_weight, router_gain)
    anywhere = pl.BlockSpec(memory_space=pl.ANY)
    vmem = pl.BlockSpec(memory_space=pltpu.VMEM)
    dma = pltpu.SemaphoreType.DMA
    serve = jax.ShapeDtypeStruct((experts, rows * n, width), jnp.bfloat16)
    scale = jax.ShapeDtypeStruct((experts, width), jnp.float32)
    og, ou, sg, su, rt = pl.pallas_call(
        functools.partial(kernel, n, banks),
        out_shape=(serve, serve, scale, scale, jax.ShapeDtypeStruct((banks, heads, depth * n), jnp.bfloat16)),
        in_specs=[anywhere, anywhere, vmem, vmem],
        out_specs=(anywhere, anywhere, vmem, vmem, vmem),
        scratch_shapes=[
            pltpu.VMEM((2, SLOTS, rows, cols), jnp.float32),
            pltpu.VMEM((2, rows, cols), jnp.float32),
            pltpu.VMEM((2, experts, n, rows, width), jnp.bfloat16),
            pltpu.VMEM((n, experts, 2, 1, cols), jnp.float32),
            pltpu.VMEM((1, cols), jnp.float32),
            dma((2, SLOTS)), dma((2,)), dma((2,)), dma((2, n)), dma((2, n)),
            dma((3, n)), dma((3, n)), dma((n,)), dma((n,)), dma((banks,)), dma((banks,)),
        ],
        compiler_params=pltpu.CompilerParams(
            collective_id=0, has_side_effects=True, vmem_limit_bytes=58 * 1024 * 1024
        ),
    )(w_gate, w_up, router_weight.T, router_gain[None, :])
    return og, ou, sg, su, rt.reshape(banks * heads, depth * n).T


def solution(mesh):
    n, banks = mesh.shape["zero"], mesh.shape["bank"]
    return jax.shard_map(
        functools.partial(local, n, banks),
        mesh=mesh,
        in_specs=(
            P(("trial", "bank"), "zero", None),
            P(("trial", "bank"), "zero", None),
            P(("trial", "zero"), "bank"),
            P(("trial", "zero")),
        ),
        out_specs=(
            P(("trial", "bank"), None, "zero"),
            P(("trial", "bank"), None, "zero"),
            P(("trial", "bank"), "zero"),
            P(("trial", "bank"), "zero"),
            P("trial", None),
        ),
        check_vma=False,
    )
```

time: 902 us -> 771 us (0.85)
  Pallas kernels: 0 us -> 745 us
  blocking collectives: 377 us -> 0 us
  waiting for transfers between devices: 312 us -> 0 us
  local copies, waits for them, and re-layouts: 123 us -> 24.9 us
  other arithmetic: 58.3 us -> 0 us
  starting transfers between devices: 14.1 us -> 0 us
  between operations: 14.1 us -> 0.65 us
    pallas_call x0 -> x1, Pallas kernels: none -> 745 us  [local(): pl.pallas_call(functools.partial(kernel, n, banks), out_shape=(serve, ser...]
    all_gather x2 -> x0, blocking collectives: 377 us -> none  [the longest x1 368 us: local(): row_router = lax.all_gather(part_router, 'zero', axis=0, tiled=True)]
    all_to_all x2 -> x0, waiting for transfers between devices: 309 us -> none  [the longest x1 309 us: local(): lax.all_to_all(narrow_up, 'zero', split_axis=2, concat_axis=1, tiled=True)]
    all_to_all x2 -> x0, local copies, waits for them, and re-layouts: 52.3 us -> none  [the longest x1 26.2 us: local(): lax.all_to_all(narrow_gate, 'zero', split_axis=2, concat_axis=1, tiled=True)]
    unnamed x9 -> x13, local copies, waits for them, and re-layouts: 69.1 us -> 24.9 us
    convert_element_type x3 -> x0, other arithmetic: 35.3 us -> none  [the longest x1 17.7 us: local(): (w_gate / jnp.expand_dims(scale_gate, 1)).astype(jnp.bfloat16)]
    reduce_sum x1 -> x0, other arithmetic: 22.1 us -> none  [local(): jnp.sum(jnp.abs(w_up), axis=1)]
    all_to_all x2 -> x0, starting transfers between devices: 14.1 us -> none  [the longest x1 7.09 us: local(): lax.all_to_all(narrow_up, 'zero', split_axis=2, concat_axis=1, tiled=True)]
  transfers between devices with their start and end apart: 3 -> 0, of which waited for: 2 -> 0; matrix products, arithmetic and copies ran while one was open for 13% -> 0% of each run, Pallas kernels for 0% -> 0%
where the time goes in v1:
time: 771 us
  Pallas kernels  745 us (97%)
  local copies, waits for them, and re-layouts  24.9 us (3%)
    pallas_call x1, Pallas kernels, local(): pl.pallas_call(functools.partial(kernel, n, banks), out_shape=(serve, ser...  745 us
    unnamed x13, local copies, waits for them, and re-layouts  24.9 us

profile of v1, /device:TPU:0, one launch (start us, length us, event | category | flops | bytes accessed | tf_op | source)
XLA Modules:
  0.0 770.7 jit_solution(10626055120075795842)
XLA Ops:
  0.6 745.1 %shard_map.83 = (bf16[16,2048,256]{2,1,0:T(8,128)(2,1)}, bf16[16,2048,256]{2,1,0:T(8,128)(2,1)}, f32[16,256]{1,0:T(8,128)}, f32[16,256]{1,0:T(8,128)}, bf16[4,16,2048]{2,1,0:T(8,128)(2,1)}) custom-call(f32[16,512,1024]{2,1,0:T(8,128)} %wg_ref.1, f32[16,512,1024]{2,1,0:T(8,128)} %wu_ref.1, f32[16,512]{1,0:T(8,128)} %bitcast.6, f32[1,512]{1,0:T(1,128)} %bitcast.7), custom_call_target="tpu_custom_call" | custom-call | tf_op jit(solution)/shard_map/pallas_call | solution.py:257
  745.7 0.0 copy-start
  745.7 14.6 %copy.14 = bf16[16,2048,256]{2,1,0:T(8,128)(2,1)} copy(bf16[16,2048,256]{2,1,0:T(8,128)(2,1)} %get-tuple-element.20) | data formatting | bytes 33554432
  760.3 2.3 copy-done
  762.6 0.0 copy-start.3
  762.6 0.0 copy-start.2
  762.6 0.0 copy-start.1
  762.6 6.2 copy.15
  768.8 0.0 copy-done.3
  768.8 0.6 copy.16
  769.4 0.0 copy-done.2
  769.4 0.6 copy.17
  770.0 0.0 copy-done.1
  770.0 0.7 copy.18
Async XLA Ops:
  745.7 16.9 %copy-start = (bf16[16,2048,256]{2,1,0:T(8,128)(2,1)S(1)}, bf16[16,2048,256]{2,1,0:T(8,128)(2,1)}, u32[]{:S(2)}) copy-start(bf16[16,2048,256]{2,1,0:T(8,128)(2,1)} %get-tuple-element.21) | copy-start | bytes 50331652
  762.6 6.2 copy-start.3
  762.6 6.8 copy-start.2
  762.6 7.4 copy-start.1

commit v2 on v1

--- a/solution.py
+++ b/solution.py
@@ -31,17 +31,21 @@
 
 
 def kernel(
-    n, banks, wg_ref, wu_ref, rw_ref, rg_ref,
-    og_ref, ou_ref, sg_ref, su_ref, rt_ref,
-    stage, first, sendbuf, parts, scales,
-    in_sem, first_sem, own_sem, send_sem, recv_sem, x_send, x_recv, rz_send, rz_recv, rb_send, rb_recv,
+    n, banks, wg_ref, wu_ref, rw_ref, rg_ref, *refs
 ):
+    og_ref, ou_ref, sg_ref, su_ref, rt_ref = refs[:5]
+    tails = refs[5 : 5 + n]
+    stage, first, sendbuf, parts, scales = refs[5 + n : 10 + n]
+    (
+    tail_sem, in_sem, first_sem, own_sem, send_sem, recv_sem, x_send, x_recv, rz_send, rz_recv, rb_send, rb_recv,
+    ) = refs[10 + n :]
     me = lax.axis_index("zero")
     bank = lax.axis_index("bank")
     w, o, so = (wg_ref, wu_ref), (og_ref, ou_ref), (sg_ref, su_ref)
     experts, rows, cols = wg_ref.shape
     width = cols // n
     d_model = rows * n
+    last = experts - 1
 
     for m in range(2):
         pltpu.make_async_copy(w[m].at[0], first.at[m], first_sem.at[m]).start()
@@ -186,6 +190,11 @@
 
     arrived(2)
 
+    def put(m, d):
+        return pltpu.make_async_copy(
+            sendbuf.at[m, last, lax.rem(me + d, n)], tails[d].at[m], tail_sem.at[d, m]
+        )
+
     def narrowed(e, carry):
         slot = e % SLOTS
         for m in range(2):
@@ -196,11 +205,16 @@
             def _():
                 load(m, e + SLOTS, slot).start()
 
-            send_at(m, e, 1)
-            keep(m, e)
+            @pl.when(e < last)
+            def _():
+                send_at(m, e, 1)
+                keep(m, e)
         return carry
 
     lax.fori_loop(1, experts, narrowed, 0)
+    for m in range(2):
+        for d in range(n):
+            put(m, d).start()
 
     def far(e, carry):
         for m in range(2):
@@ -208,7 +222,10 @@
                 send_at(m, e, t)
         return carry
 
-    lax.fori_loop(1, experts, far, 0)
+    lax.fori_loop(1, last, far, 0)
+    for m in range(2):
+        for d in range(n):
+            put(m, d).wait()
 
     others("zero", me, n, lambda p: row_copy(p, p).wait_recv())
 
@@ -229,49 +246,105 @@
     for m in range(2):
         def whole(s, p):
             return pltpu.make_async_remote_copy(
-                src_ref=sendbuf.at[m, :, p],
+                src_ref=sendbuf.at[m, pl.ds(0, last), p],
                 dst_ref=o[m].at[:, pl.ds(pl.multiple_of(s * rows, rows), rows), :],
                 send_sem=send_sem.at[m, p], recv_sem=recv_sem.at[m, s],
                 device_id={"zero": p}, device_id_type=MESH,
             )
 
         pltpu.make_async_copy(
-            sendbuf.at[m, :, me], o[m].at[:, pl.ds(pl.multiple_of(me * rows, rows), rows), :], own_sem.at[m]
+            sendbuf.at[m, pl.ds(0, last), me], o[m].at[:, pl.ds(pl.multiple_of(me * rows, rows), rows), :], own_sem.at[m]
         ).wait()
         others("zero", me, n, lambda p: whole(me, p).wait_send())
         others("zero", me, n, lambda p: whole(p, p).wait_recv())
+
+
+def copy_kernel(a_ref, b_ref, c_ref, d_ref):
+    c_ref[...] = a_ref[...]
+    d_ref[...] = b_ref[...]
+
+
+def spread(experts, og, ou):
+    main, height, width = og.shape
+    block = pl.BlockSpec((1, height, width), lambda e: (e, 0, 0))
+    out = jax.ShapeDtypeStruct((experts, height, width), og.dtype)
+    return pl.pallas_call(
+        copy_kernel,
+        grid=(main,),
+        in_specs=[block, block],
+        out_specs=(block, block),
+        out_shape=(out, out),
+        cost_estimate=pl.CostEstimate(flops=0, bytes_accessed=8 * og.size, transcendentals=0),
+        name="spread",
+    )(og, ou)
+
+
+def join_kernel(n, a_ref, b_ref, *refs):
+    blocks, outs, sem = refs[:n], refs[n : n + 2], refs[n + 2]
+    me = lax.axis_index("zero")
+    last = outs[0].shape[0] - 1
+    rows = blocks[0].shape[1]
+    copies = []
+    for d in range(n):
+        at = pl.ds(pl.multiple_of(lax.rem(me - d + n, n) * rows, rows), rows)
+        for m in range(2):
+            copies.append(pltpu.make_async_copy(blocks[d].at[m], outs[m].at[last, at, :], sem.at[d, m]))
+    for copy in copies:
+        copy.start()
+    for copy in copies:
+        copy.wait()
+
+
+def join(n, og, ou, blocks):
+    anywhere = pl.BlockSpec(memory_space=pl.ANY)
+    vmem = pl.BlockSpec(memory_space=pltpu.VMEM)
+    return pl.pallas_call(
+        functools.partial(join_kernel, n),
+        out_shape=(jax.ShapeDtypeStruct(og.shape, og.dtype), jax.ShapeDtypeStruct(ou.shape, ou.dtype)),
+        in_specs=[anywhere, anywhere] + [vmem] * n,
+        out_specs=(anywhere, anywhere),
+        scratch_shapes=[pltpu.SemaphoreType.DMA((n, 2))],
+        input_output_aliases={0: 0, 1: 1},
+        name="join",
+    )(og, ou, *blocks)
 
 
 def local(n, banks, w_gate, w_up, router_weight, router_gain):
     experts, rows, cols = w_gate.shape
     width = cols // n
     depth, heads = router_weight.shape
-    fits = width % 128 == 0 and rows % 16 == 0 and depth % 128 == 0 and heads % 16 == 0 and experts > 1
+    fits = width % 128 == 0 and rows % 16 == 0 and depth % 128 == 0 and heads % 16 == 0 and experts > 2
     if not fits:
         return plain(n, w_gate, w_up, router_weight, router_gain)
     anywhere = pl.BlockSpec(memory_space=pl.ANY)
     vmem = pl.BlockSpec(memory_space=pltpu.VMEM)
     dma = pltpu.SemaphoreType.DMA
-    serve = jax.ShapeDtypeStruct((experts, rows * n, width), jnp.bfloat16)
+    serve = jax.ShapeDtypeStruct((experts - 1, rows * n, width), jnp.bfloat16)
+    tail = jax.ShapeDtypeStruct((2, rows, width), jnp.bfloat16)
     scale = jax.ShapeDtypeStruct((experts, width), jnp.float32)
-    og, ou, sg, su, rt = pl.pallas_call(
+    og, ou, sg, su, rt, *tails = pl.pallas_call(
         functools.partial(kernel, n, banks),
-        out_shape=(serve, serve, scale, scale, jax.ShapeDtypeStruct((banks, heads, depth * n), jnp.bfloat16)),
+        out_shape=(serve, serve, scale, scale, jax.ShapeDtypeStruct((banks, heads, depth * n), jnp.bfloat16), *[tail] * n),
         in_specs=[anywhere, anywhere, vmem, vmem],
-        out_specs=(anywhere, anywhere, vmem, vmem, vmem),
+        out_specs=(anywhere, anywhere, vmem, vmem, vmem, *[anywhere] * n),
         scratch_shapes=[
             pltpu.VMEM((2, SLOTS, rows, cols), jnp.float32),
             pltpu.VMEM((2, rows, cols), jnp.float32),
             pltpu.VMEM((2, experts, n, rows, width), jnp.bfloat16),
             pltpu.VMEM((n, experts, 2, 1, cols), jnp.float32),
             pltpu.VMEM((1, cols), jnp.float32),
-            dma((2, SLOTS)), dma((2,)), dma((2,)), dma((2, n)), dma((2, n)),
+            dma((n, 2)), dma((2, SLOTS)), dma((2,)), dma((2,)), dma((2, n)), dma((2, n)),
             dma((3, n)), dma((3, n)), dma((n,)), dma((n,)), dma((banks,)), dma((banks,)),
         ],
         compiler_params=pltpu.CompilerParams(
             collective_id=0, has_side_effects=True, vmem_limit_bytes=58 * 1024 * 1024
         ),
     )(w_gate, w_up, router_weight.T, router_gain[None, :])
+    arrived = [tails[0]] + [
+        lax.ppermute(tails[d], "zero", [(i, (i + d) % n) for i in range(n)]) for d in range(1, n)
+    ]
+    og, ou = spread(experts, og, ou)
+    og, ou = join(n, og, ou, arrived)
     return og, ou, sg, su, rt.reshape(banks * heads, depth * n).T
 
 

time: 771 us -> 752 us (0.975); the launches traced: 771 us -> 744 us
  local copies, waits for them, and re-layouts: 24.9 us -> 2.91 us
  Pallas kernels: 745 us -> 729 us
    pallas_call x1, Pallas kernels: 745 us -> 700 us  [local(): pl.pallas_call(functools.partial(kernel, n, banks), out_shape=(serve, ser...]
    pallas_call x0 -> x2, Pallas kernels: none -> 29.1 us  [the longest x1 26.2 us: spread(): pl.pallas_call(copy_kernel, grid=(main,), in_specs=[block, block], out_sp...]
    unnamed x13 -> x15, local copies, waits for them, and re-layouts: 24.9 us -> 2.91 us
  transfers between devices with their start and end apart: 0 -> 3, of which waited for: 0 -> 1; matrix products, arithmetic and copies ran while one was open for 0% -> 0% of each run, Pallas kernels for 0% -> 4%
where the time goes in v2:
time: 752 us; the launch traced here: 744 us
  Pallas kernels  729 us (97%)
    pallas_call x1, Pallas kernels, local(): pl.pallas_call(functools.partial(kernel, n, banks), out_shape=(serve, ser...  700 us
    pallas_call x1, Pallas kernels, spread(): pl.pallas_call(copy_kernel, grid=(main,), in_specs=[block, block], out_sp...  26.2 us
  transfers between devices with their start and end apart: 3, of which 1 were waited for; matrix products, arithmetic and copies ran while one was open for 0% of the time, Pallas kernels for 4%

profile of v2, /device:TPU:0, one launch (start us, length us, event | category | flops | bytes accessed | tf_op | source)
XLA Modules:
  0.0 743.7 jit_solution(11767929805235893225)
XLA Ops:
  0.6 700.2 %shard_map.83 = (bf16[15,2048,256]{2,1,0:T(8,128)(2,1)}, bf16[15,2048,256]{2,1,0:T(8,128)(2,1)}, f32[16,256]{1,0:T(8,128)}, f32[16,256]{1,0:T(8,128)}, bf16[4,16...) custom-call(f32[16,512,1024]{2,1,0:T(8,128)} %wg_ref.1, ...), custom_call_target="tpu_custom_call" | custom-call | tf_op jit(solution)/shard_map/pallas_call | solution.py:325
  700.9 0.1 collective-permute-start
  700.9 2.8 collective-permute-start.1
  703.7 1.0 collective-permute-start.2
  704.8 26.2 %spread.1 = (bf16[16,2048,256]{2,1,0:T(8,128)(2,1)}, bf16[16,2048,256]{2,1,0:T(8,128)(2,1)}) custom-call(bf16[15,2048,256]{2,1,0:T(8,128)(2,1)} %get-tuple-element.18.a_ref, bf16[15,2048,256]{2,1,0:T(8,128)(2,1)} %get-tuple-element.19.b_ref), custom_call_target="tpu_custom_call" | custom-call | bytes 62914560 | tf_op jit(solution)/shard_map/spread/pallas_call | solution.py:271
  730.9 0.0 collective-permute-done.refs_1_
  730.9 0.0 copy-start
  730.9 6.9 collective-permute-done.1.refs_2_
  737.9 0.0 copy-start.1
  737.9 0.0 collective-permute-done.2.refs_3_
  737.9 0.0 copy-start.2
  737.9 0.0 copy-done
  737.9 0.8 copy-done.1
  738.6 0.2 copy-done.2
  738.8 0.0 copy-start.5
  738.8 0.0 copy-start.4
  738.8 0.0 copy-start.3
  738.8 2.9 join.1
  741.8 0.0 copy-done.5
  741.8 0.6 copy.16
  742.4 0.0 copy-done.4
  742.4 0.6 copy.17
  743.0 0.0 copy-done.3
  743.0 0.7 copy.18
Async XLA Ops:
  700.9 30.1 %collective-permute-start = (bf16[2,512,256]{2,1,0:T(8,128)(2,1)}, bf16[2,512,256]{2,1,0:T(8,128)(2,1)S(1)}, u32[]{:S(2)}, u32[]{:S(2)}) collective-permute-start(bf16[2,512,256]{2,1,0:T(8,128)(2,1)} %get-tuple-element.23), channel_id=1, source_target_pairs={{0,1},{1,2},{2,3},{3,0},{4,5},{5,6},{6,7},{7,4},{8,9},{9,10},{10,1... | collective-permute-start | bytes 1572872 | tf_op jit(solution)/shard_map/ppermute | solution.py:344
  700.9 36.9 %collective-permute-start.1 = (bf16[2,512,256]{2,1,0:T(8,128)(2,1)}, bf16[2,512,256]{2,1,0:T(8,128)(2,1)S(1)}, u32[]{:S(2)}, u32[]{:S(2)}) collective-permute-start(bf16[2,512,256]{2,1,0:T(8,128)(2,1)} %get-tuple-element.24), channel_id=1, source_target_pairs={{0,2},{1,3},{2,0},{3,1},{4,6},{5,7},{6,4},{7,5},{8,10},{9,11},{10,... | collective-permute-start | bytes 1572872 | tf_op jit(solution)/shard_map/ppermute | solution.py:344
  703.7 34.1 %collective-permute-start.2 = (bf16[2,512,256]{2,1,0:T(8,128)(2,1)}, bf16[2,512,256]{2,1,0:T(8,128)(2,1)S(1)}, u32[]{:S(2)}, u32[]{:S(2)}) collective-permute-start(bf16[2,512,256]{2,1,0:T(8,128)(2,1)} %get-tuple-element.25), channel_id=1, source_target_pairs={{0,3},{1,0},{2,1},{3,2},{4,7},{5,4},{6,5},{7,6},{8,11},{9,8},{10,9... | collective-permute-start | bytes 1572872 | tf_op jit(solution)/shard_map/ppermute | solution.py:344
  730.9 6.9 copy-start
  737.9 0.8 copy-start.1
  737.9 1.0 copy-start.2
  738.8 2.9 copy-start.5
  738.8 3.6 copy-start.4
  738.8 4.2 copy-start.3
